TPU v7x, 32 devices: a whole 2x2x4 slice. The times are simulated.
32 devices in a mesh: row: 8 (over z, x), col: 4 (over y, core).
Axes of the slice: x: 2, y: 2, z: 4, core: 2. Of those that a mesh axis runs over, the one named last changes fastest.
Arguments:
- voltage: float32 [2, 4096, 16384], P(None, ('row', 'col')), may hold values from -6 to 6
- chirp_phase: float32 [16384, 4096], P(('row', 'col')), may hold values from -3.140625 to 3.140625
- filter_taps: float32 [8, 1024], replicated, may hold values from -0.0625 to 0.0625
Outputs:
- filterbank: float32 [2, 1024, 65536], P(None, None, ('row', 'col'))
All inputs are finite; a program needn't handle non-finite values.
Results may differ from a plain program's by a relative error of at most 0.00015.
Values sent between devices are 32-bit elements; how exact they have to be, the bound alone decides.
A program may use at most 192 MiB of HBM per device.

v0:
```python
import math

import jax
import jax.numpy as jnp
from jax import lax
from jax.sharding import PartitionSpec as P

precise = lax.Precision.HIGHEST


def passed_along(block, axis, distance):
    devices = range(lax.axis_size(axis))
    route = [(i - distance, i) for i in devices if i - distance in devices]
    return lax.ppermute(block, axis, route)


def dft_table(radix, direction):
    digits = jnp.arange(radix, dtype=jnp.int32)
    product = digits[:, None] * digits[None, :] % radix
    turn = direction * 2.0 * math.pi / radix * product.astype(jnp.float32)
    cos_part = jnp.cos(turn)
    sin_part = jnp.sin(turn)
    upper = jnp.stack([cos_part, sin_part], axis=1)
    lower = jnp.stack([-sin_part, cos_part], axis=1)
    return jnp.stack([upper, lower], axis=0)


def complex_product(values, cos_part, sin_part):
    real_part = values[0] * cos_part - values[1] * sin_part
    imag_part = values[0] * sin_part + values[1] * cos_part
    return jnp.stack([real_part, imag_part])


def inner_twist(outer_radix, inner_radix, direction):
    outer_digits = jnp.arange(outer_radix, dtype=jnp.int32)
    inner_digits = jnp.arange(inner_radix, dtype=jnp.int32)
    length = outer_radix * inner_radix
    product = outer_digits[:, None] * inner_digits[None, :] % length
    turn = direction * 2.0 * math.pi / length * product.astype(jnp.float32)
    return (jnp.cos(turn), jnp.sin(turn))


def dft_rows(values, direction):
    length = values.shape[1]
    column_count = values.shape[2]
    inner_radix = min(length, 128)
    outer_radix = length // inner_radix
    blocked = values.reshape(2, outer_radix, inner_radix, column_count)
    partial_value = jnp.einsum(
        "cadk,cabm->dkbm", dft_table(outer_radix, direction), blocked, precision=precise
    )
    cos_part, sin_part = inner_twist(outer_radix, inner_radix, direction)
    partial_value = complex_product(partial_value, cos_part[:, :, None], sin_part[:, :, None])
    result = jnp.einsum(
        "cbdq,ckbm->dqkm", dft_table(inner_radix, direction), partial_value, precision=precise
    )
    return result.reshape(2, length, column_count)


def dft_cols(values, direction):
    length = values.shape[2]
    row_count = values.shape[1]
    inner_radix = min(length, 128)
    outer_radix = length // inner_radix
    blocked = values.reshape(2, row_count, outer_radix, inner_radix)
    partial_value = jnp.einsum(
        "cadk,cmab->dmkb", dft_table(outer_radix, direction), blocked, precision=precise
    )
    cos_part, sin_part = inner_twist(outer_radix, inner_radix, direction)
    partial_value = complex_product(partial_value, cos_part, sin_part)
    result = jnp.einsum(
        "cbdq,cmkb->dmqk", dft_table(inner_radix, direction), partial_value, precision=precise
    )
    return result.reshape(2, row_count, length)


def rotate(values, row_index, col_index, total, direction, factor):
    product = row_index[:, None] * col_index[None, :] % total
    turn = direction * 2.0 * math.pi / total * product.astype(jnp.float32)
    return complex_product(values, factor * jnp.cos(turn), factor * jnp.sin(turn))


def spread(values):
    return lax.all_to_all(values, ("row", "col"), split_axis=2, concat_axis=1, tiled=True)


def collect(values):
    return lax.all_to_all(values, ("row", "col"), split_axis=1, concat_axis=2, tiled=True)


def local(voltage, chirp_phase, filter_taps):
    device_count = lax.axis_size("row") * lax.axis_size("col")
    device = lax.axis_index(("row", "col"))
    local_rows = voltage.shape[1]
    total_rows = local_rows * device_count
    total_cols = voltage.shape[2]
    local_cols = total_cols // device_count
    total = total_rows * total_cols
    signal = spread(voltage)
    signal = dft_rows(signal, -1.0)
    row_index = jnp.arange(total_rows, dtype=jnp.int32)
    col_index = device * local_cols + jnp.arange(local_cols, dtype=jnp.int32)
    signal = rotate(signal, row_index, col_index, total, -1.0, 1.0)
    signal = collect(signal)
    signal = dft_cols(signal, -1.0)
    turned_phase = jnp.transpose(chirp_phase)
    local_phase = lax.all_to_all(
        turned_phase, ("row", "col"), split_axis=0, concat_axis=1, tiled=True
    )
    signal = complex_product(signal, jnp.cos(local_phase), jnp.sin(local_phase))
    signal = dft_cols(signal, 1.0)
    row_index = device * local_rows + jnp.arange(local_rows, dtype=jnp.int32)
    col_index = jnp.arange(total_cols, dtype=jnp.int32)
    signal = rotate(signal, row_index, col_index, total, 1.0, 1.0 / total)
    signal = spread(signal)
    signal = dft_rows(signal, 1.0)
    signal = collect(signal)
    tap_count = filter_taps.shape[0]
    channel_count = filter_taps.shape[1]
    samples = signal.reshape(2, local_rows * total_cols)
    frame_count = samples.shape[1] // channel_count
    frames = samples.reshape(2, frame_count, channel_count)
    history = passed_along(frames[:, frame_count - tap_count + 1 :, :], ("row", "col"), 1)
    extended = jnp.concatenate([history, frames], axis=1)
    turned = jnp.transpose(extended, (0, 2, 1))
    weighted = jnp.zeros((2, channel_count, frame_count), jnp.float32)
    for tap_delay in range(tap_count):
        offset = tap_count - 1 - tap_delay
        weighted = (
            weighted
            + filter_taps[tap_delay][None, :, None] * turned[:, :, offset : offset + frame_count]
        )
    return dft_rows(weighted, -1.0)


def solution(mesh):
    in_specs = (P(None, ("row", "col"), None), P(("row", "col"), None), P())
    out_specs = P(None, None, ("row", "col"))
    return jax.shard_map(local, mesh=mesh, in_specs=in_specs, out_specs=out_specs, check_vma=False)
```

profile of v0, /device:TPU:6, one launch (start us, length us, event | category | flops | bytes accessed | tf_op | source)
XLA Modules:
  0.0 2393.4 jit_solution(8709069159866349502)
XLA Ops:
  0.0 24.9 %copy.169 = f32[2,128,16384]{1,0,2:T(2,128)} copy(f32[2,128,16384]{2,1,0:T(8,128)} %param.3) | data formatting | bytes 33554432 | tf_op args[0]
  24.9 6.1 all-to-all-start
  31.0 9.1 copy.181
  40.1 370.0 %all-to-all-done = f32[2,128,16384]{1,0,2:T(2,128)} async-done(((f32[2,128,16384]{1,0,2:T(2,128)}), f32[2,128,16384]{1,0,2:T(2,128)}, u32[]{:S(2)}, u32[]{:S(2)}) %all-to-all-start) | async-done | bytes 16777248 | tf_op jit(solution)/shard_map/all_to_all | solution.py:84
  410.1 3.4 all-to-all-start.2
  414.6 20.2 copy.234
  434.8 21.7 fusion.71
  456.5 7.0 multiply_subtract_fusion.5
  463.5 3.3 pad_maximum_fusion
  466.8 28.9 %fusion.59 = f32[2,128,32,512]{3,1,2,0:T(8,128)S(1)} fusion(f32[2,32,128,512]{3,1,2,0:T(8,128)S(1)} %pad_maximum_fusion, f32[1,128,2,128]{1,3,0,2:T(8,128)S(1)} %get-tuple-element.30, f32[1,128,2,128]{1,3,0,2:T(8,128)S(1)} %get-tuple-element.29), kind=kOutput, calls=%fused_computation.103 | convolution fusion | flops 12884967424 | bytes 33816576 | tf_op jit(solution)/shard_map/cbdq,ckbm->dqkm/dot_general | solution.py:54
  495.7 7.0 fusion.139
  502.7 8.2 copy.172
  511.0 8.2 copy.173
  519.2 36.9 %fusion.51 = (f32[1,4096,512]{2,1,0:T(8,128)S(1)}, f32[1,4096,512]{2,1,0:T(8,128)S(1)}) fusion(f32[1,128,32,512]{3,2,1,0:T(8,128)S(1)} %copy.173, f32[1,128,32,512]{3,2,1,0:T(8,128)S(1)} %copy.172, s32[512]{0:T(512)S(1)} %iota_add_fusion), kind=kLoop, calls=%fused_computation.77 | loop fusion | flops 41943040 | bytes 33556480 | tf_op jit(solution)/shard_map/sub | solution.py:29
  556.1 1.8 pad_maximum_fusion.1
  557.9 32.2 %copy.174 = f32[2,4096,512]{2,0,1:T(2,128)} copy(f32[2,4096,512]{2,1,0:T(8,128)S(1)} %pad_maximum_fusion.1) | data formatting | bytes 33554432 | tf_op jit(solution)/shard_map/stack | solution.py:31
  590.2 11.6 all-to-all-done.2
  601.7 5.0 all-to-all-start.1
  607.9 31.5 %sine_bitcast_fusion = (f32[128,32,512]{2,0,1:T(8,128)}, f32[128,32,512]{2,0,1:T(8,128)}) fusion(f32[32,128,512]{2,1,0:T(8,128)} %all-to-all-done.2), kind=kLoop, calls=%fused_computation.93 | loop fusion | bytes 25165824 | tf_op jit(solution)/shard_map/sin | solution.py:110
  639.4 9.0 copy.182
  648.4 9.4 copy.183
  657.8 8.9 copy.184
  666.7 9.4 copy.185
  676.1 309.5 %all-to-all-done.1 = f32[2,4096,512]{2,0,1:T(2,128)} async-done(((f32[2,4096,512]{2,0,1:T(2,128)}), f32[2,4096,512]{2,0,1:T(2,128)}, u32[]{:S(2)}, u32[]{:S(2)}) %all-to-all-start.1) | async-done | bytes 16777248 | tf_op jit(solution)/shard_map/all_to_all | solution.py:88
  985.5 14.2 copy.175
  999.7 17.5 copy.176
  1017.2 18.1 copy.211
  1035.3 17.1 convolution_bitcast_fusion
  1052.4 7.0 multiply_subtract_fusion.4
  1059.4 31.5 %fusion.36 = f32[2,128,128,128]{2,3,0,1:T(8,128)} fusion(f32[1,128,128,128]{2,3,0,1:T(8,128)} %get-tuple-element.14, f32[1,128,128,128]{2,3,0,1:T(8,128)} %get-tuple-element.13, f32[1,128,2,128]{1,3,0,2:T(8,128)S(1)} %get-tuple-element.30, f32[1,128,2,128]{1,3,0,2:T(8,128)S(1)} %get-tuple-element.29), kind=kOutput, calls=%fused_computation.59 | convolution fusion | flops 12889161728 | bytes 33816576 | tf_op jit(solution)/shard_map/cbdq,cmkb->dmqk/dot_general | solution.py:71
  1090.9 19.0 multiply_subtract_fusion.3
  1109.8 17.3 fusion.37
  1127.2 7.1 multiply_subtract_fusion.2
  1134.3 31.7 %fusion.40 = f32[2,128,128,128]{2,3,0,1:T(8,128)S(1)} fusion(f32[1,128,128,128]{2,3,0,1:T(8,128)} %get-tuple-element.12, f32[1,128,128,128]{2,3,0,1:T(8,128)} %get-tuple-element.11, f32[1,128,2,128]{1,3,2,0:T(8,128)S(1)} %get-tuple-element.28, f32[1,128,2,128]{1,3,2,0:T(8,128)S(1)} %get-tuple-element.27), kind=kOutput, calls=%fused_computation.61 | convolution fusion | flops 12889161728 | bytes 33816576 | tf_op jit(solution)/shard_map/cbdq,cmkb->dmqk/dot_general | solution.py:71
  1166.0 6.8 fusion.138
  1172.8 9.4 copy.191
  1182.2 9.3 copy.192
  1191.5 36.6 %fusion.49 = (f32[1,128,16384]{1,2,0:T(8,128)S(1)}, f32[1,128,16384]{1,2,0:T(8,128)S(1)}) fusion(f32[1,128,128,128]{1,3,2,0:T(8,128)} %copy.192, f32[1,128,128,128]{1,3,2,0:T(8,128)} %copy.191, s32[128]{0:T(128)S(1)} %iota_add_fusion.1), kind=kLoop, calls=%fused_computation.71 | loop fusion | flops 46137344 | bytes 33554944 | tf_op jit(solution)/shard_map/sub | solution.py:29
  1228.1 1.2 pad_maximum_fusion.2
  1229.2 61.7 %copy.193 = f32[2,128,16384]{1,0,2:T(2,128)} copy(f32[2,128,16384]{1,2,0:T(8,128)S(1)} %pad_maximum_fusion.2) | data formatting | bytes 33554432 | tf_op jit(solution)/shard_map/stack | solution.py:31
  1291.0 4.0 all-to-all-start.3
  1295.5 377.9 %all-to-all-done.3 = f32[2,128,16384]{1,0,2:T(2,128)} async-done(((f32[2,128,16384]{1,0,2:T(2,128)}), f32[2,128,16384]{1,0,2:T(2,128)}, u32[]{:S(2)}, u32[]{:S(2)}) %all-to-all-start.3) | async-done | bytes 16777248 | tf_op jit(solution)/shard_map/all_to_all | solution.py:84
  1673.4 20.1 copy.247
  1693.4 21.7 fusion.74
  1715.2 7.0 multiply_subtract_fusion.1
  1722.2 3.3 pad_maximum_fusion.3
  1725.4 28.9 %fusion.62 = f32[2,128,32,512]{3,1,2,0:T(8,128)S(1)} fusion(f32[2,32,128,512]{3,1,2,0:T(8,128)S(1)} %pad_maximum_fusion.3, f32[1,128,2,128]{1,3,2,0:T(8,128)S(1)} %get-tuple-element.28, f32[1,128,2,128]{1,3,2,0:T(8,128)S(1)} %get-tuple-element.27), kind=kOutput, calls=%fused_computation.104 | convolution fusion | flops 12884967424 | bytes 33816576 | tf_op jit(solution)/shard_map/cbdq,ckbm->dqkm/dot_general | solution.py:54
  1754.3 20.1 copy.198
  1774.4 28.6 %copy.199 = f32[2,4096,512]{2,0,1:T(2,128)} copy(f32[2,4096,512]{2,1,0:T(8,128)} %bitcast.229) | data formatting | bytes 33554432 | tf_op jit(solution)/shard_map/reshape | solution.py:57
  1803.0 3.8 all-to-all-start.4
  1807.3 377.8 %all-to-all-done.4 = f32[2,4096,512]{2,0,1:T(2,128)} async-done(((f32[2,4096,512]{2,0,1:T(2,128)}), f32[2,4096,512]{2,0,1:T(2,128)}, u32[]{:S(2)}, u32[]{:S(2)}) %all-to-all-start.4) | async-done | bytes 16777248 | tf_op jit(solution)/shard_map/all_to_all | solution.py:88
  2185.1 17.8 copy.279
  2202.9 19.2 reshape_reshape.3
  2222.1 0.8 slice.168
  2222.9 1.9 collective-permute-start
  2225.0 3.5 collective-permute-done
  2228.5 11.8 maximum_bitcast_fusion
  2240.3 50.0 %fusion = f32[2,1024,2048]{1,2,0:T(8,128)} fusion(f32[2,1024,2055]{1,2,0:T(8,128)} %maximum_bitcast_fusion, f32[1024]{0:T(1024)S(1)} %bitcast.241, f32[1024]{0:T(1024)S(1)} %bitcast.242, f32[1024]{0:T(1024)S(1)} %bitcast.236, f32[1024]{0:T(1024)S(1)} %bitcast.237, f32[1024]{0:T(1024)S(1)} %bitcast.238, f32[1024]{0:T(1024)S(1)} %bitcast.239, ...), kind=kLoop, calls=%fused_computation.2 | loop fusion | flops 62914560 | bytes 151027712 | tf_op jit(solution)/shard_map/add | solution.py:130
  2290.3 17.3 copy.201
  2307.7 32.0 %fusion.65 = f32[2,8,128,2048]{3,1,2,0:T(8,128)} fusion(f32[2,8,128,2048]{3,2,1,0:T(8,128)} %bitcast.231, f32[1,8,2,8]{1,3,0,2:T(8,128)S(1)} %copy.167, f32[1,8,2,8]{1,3,0,2:T(8,128)S(1)} %copy.166), kind=kOutput, calls=%fused_computation.105 | convolution fusion | flops 805306624 | bytes 33555456 | tf_op jit(solution)/shard_map/cadk,cabm->dkbm/dot_general | solution.py:49
  2339.7 7.2 multiply_subtract_fusion
  2347.0 2.0 pad_maximum_fusion.4
  2349.0 23.7 fusion.68
  2372.7 20.2 copy.278
  (38 shorter events, 3.2 us)
Async XLA Ops:
  24.9 385.2 %all-to-all-start = ((f32[2,128,16384]{1,0,2:T(2,128)}), f32[2,128,16384]{1,0,2:T(2,128)}, u32[]{:S(2)}, u32[]{:S(2)}) async-start(f32[2,128,16384]{1,0,2:T(2,128)} %copy.169), calls=%async_computation | async-start | bytes 33554432 | tf_op jit(solution)/shard_map/all_to_all | solution.py:84
  410.1 191.6 %all-to-all-start.2 = ((f32[32,128,512]{2,1,0:T(8,128)}), f32[32,128,512]{2,1,0:T(8,128)}, u32[]{:S(2)}, u32[]{:S(2)}) async-start(f32[32,128,512]{2,1,0:T(8,128)} %bitcast.232), calls=%async_computation.2 | async-start | bytes 16777216 | tf_op jit(solution)/shard_map/all_to_all | solution.py:107
  414.6 644.8 %copy-start = (f32[1,128,2,128]{1,3,0,2:T(8,128)}, f32[1,128,2,128]{1,3,0,2:T(8,128)S(1)}, u32[]{:S(2)}) copy-start(f32[1,128,2,128]{1,3,0,2:T(8,128)S(1)} %get-tuple-element.29) | copy-start | bytes 393220
  414.6 644.8 %copy-start.2 = (f32[1,128,2,128]{1,3,0,2:T(8,128)}, f32[1,128,2,128]{1,3,0,2:T(8,128)S(1)}, u32[]{:S(2)}) copy-start(f32[1,128,2,128]{1,3,0,2:T(8,128)S(1)} %get-tuple-element.30) | copy-start | bytes 393220
  601.7 383.8 %all-to-all-start.1 = ((f32[2,4096,512]{2,0,1:T(2,128)}), f32[2,4096,512]{2,0,1:T(2,128)}, u32[]{:S(2)}, u32[]{:S(2)}) async-start(f32[2,4096,512]{2,0,1:T(2,128)} %copy.174), calls=%async_computation.1 | async-start | bytes 33554432 | tf_op jit(solution)/shard_map/all_to_all | solution.py:88
  1291.0 382.4 %all-to-all-start.3 = ((f32[2,128,16384]{1,0,2:T(2,128)}), f32[2,128,16384]{1,0,2:T(2,128)}, u32[]{:S(2)}, u32[]{:S(2)}) async-start(f32[2,128,16384]{1,0,2:T(2,128)} %copy.193), calls=%async_computation.3 | async-start | bytes 33554432 | tf_op jit(solution)/shard_map/all_to_all | solution.py:84
  1803.0 4.2 copy-start.4
  1803.0 382.1 %all-to-all-start.4 = ((f32[2,4096,512]{2,0,1:T(2,128)}), f32[2,4096,512]{2,0,1:T(2,128)}, u32[]{:S(2)}, u32[]{:S(2)}) async-start(f32[2,4096,512]{2,0,1:T(2,128)} %copy.199), calls=%async_computation.4 | async-start | bytes 33554432 | tf_op jit(solution)/shard_map/all_to_all | solution.py:88
  2222.9 5.6 collective-permute-start
  2346.9 2.0 copy-start.1
  2346.9 2.0 copy-start.3
where the time goes:
time: 2410 us; the launch traced here: 2390 us
  waiting for transfers between devices  1450 us (60%)
  local copies, waits for them, and re-layouts  460 us (19%)
  matrix products  255 us (11%)
  other arithmetic  204 us (8%)
  starting transfers between devices  24.3 us (1%)
    all_to_all x2, waiting for transfers between devices, spread(): lax.all_to_all(values, ('row', 'col'), split_axis=2, concat_axis=1, tiled...  748 us
    all_to_all x2, waiting for transfers between devices, collect(): lax.all_to_all(values, ('row', 'col'), split_axis=1, concat_axis=2, tiled...  687 us
    sub x8, other arithmetic, complex_product(): real_part = values[0] * cos_part - values[1] * sin_part  128 us
    another operation x2, local copies, waits for them, and re-layouts, complex_product(): return jnp.stack([real_part, imag_part])  94 us
    dot_general x3, matrix products, dft_rows(): jnp.einsum('cbdq,ckbm->dqkm', dft_table(inner_radix, direction), partial_...  81.5 us
    dot_general x3, matrix products, dft_rows(): jnp.einsum('cadk,cabm->dkbm', dft_table(outer_radix, direction), blocked,...  75.5 us
    dot_general x2, matrix products, dft_cols(): jnp.einsum('cbdq,cmkb->dmqk', dft_table(inner_radix, direction), partial_...  63.2 us
    add x1, other arithmetic, local(): weighted + filter_taps[tap_delay][None, :, None] * turned[:, :, offset:of...  50 us
  transfers between devices with their start and end apart: 6, of which 6 were waited for; matrix products, arithmetic and copies ran while one was open for 11% of the time, Pallas kernels for 0%

commit v1 on v0

--- a/solution.py
+++ b/solution.py
@@ -5,7 +5,7 @@
 from jax import lax
 from jax.sharding import PartitionSpec as P
 
-precise = lax.Precision.HIGHEST
+precise = lax.Precision.HIGH
 
 
 def passed_along(block, axis, distance):
@@ -74,10 +74,52 @@
     return result.reshape(2, row_count, length)
 
 
-def rotate(values, row_index, col_index, total, direction, factor):
-    product = row_index[:, None] * col_index[None, :] % total
+def unit_table(left_index, right_index, total, direction, factor):
+    product = left_index[:, None] * right_index[None, :] % total
     turn = direction * 2.0 * math.pi / total * product.astype(jnp.float32)
-    return complex_product(values, factor * jnp.cos(turn), factor * jnp.sin(turn))
+    return factor * jnp.cos(turn), factor * jnp.sin(turn)
+
+
+def rotate(values, row_start, row_count, col_start, col_count, total, direction, factor):
+    split_rows = row_count >= col_count
+    long_count = row_count if split_rows else col_count
+    long_start = row_start if split_rows else col_start
+    short_count = col_count if split_rows else row_count
+    short_start = col_start if split_rows else row_start
+    fine = min(long_count, 128)
+    short_index = short_start + jnp.arange(short_count, dtype=jnp.int32)
+    coarse_index = long_start + fine * jnp.arange(long_count // fine, dtype=jnp.int32)
+    fine_index = jnp.arange(fine, dtype=jnp.int32)
+    tables = (
+        unit_table(coarse_index, short_index, total, direction, factor),
+        unit_table(fine_index, short_index, total, direction, 1.0),
+    )
+    if split_rows:
+        blocked = values.reshape(2, long_count // fine, fine, short_count)
+        (cc, cs), (fc, fs) = tables
+        cc, cs, fc, fs = cc[:, None, :], cs[:, None, :], fc[None], fs[None]
+    else:
+        blocked = values.reshape(2, short_count, long_count // fine, fine)
+        (cc, cs), (fc, fs) = tables
+        cc, cs = cc.T[:, :, None], cs.T[:, :, None]
+        fc, fs = fc.T[:, None, :], fs.T[:, None, :]
+    turned = complex_product(blocked, cc * fc - cs * fs, cc * fs + cs * fc)
+    return turned.reshape(values.shape)
+
+
+def unit_phase(phase):
+    half = 0.5 * phase
+    square = half * half
+    sine = half * polynomial(square, (1, -6, 120, -5040, 362880, -39916800, 6227020800))
+    cosine = polynomial(square, (1, -2, 24, -720, 40320, -3628800, 479001600))
+    return 1.0 - 2.0 * sine * sine, 2.0 * sine * cosine
+
+
+def polynomial(square, factorials):
+    result = jnp.full_like(square, 1.0 / factorials[-1])
+    for factorial in factorials[-2::-1]:
+        result = result * square + 1.0 / factorial
+    return result
 
 
 def spread(values):
@@ -98,20 +140,20 @@
     total = total_rows * total_cols
     signal = spread(voltage)
     signal = dft_rows(signal, -1.0)
-    row_index = jnp.arange(total_rows, dtype=jnp.int32)
-    col_index = device * local_cols + jnp.arange(local_cols, dtype=jnp.int32)
-    signal = rotate(signal, row_index, col_index, total, -1.0, 1.0)
+    signal = rotate(
+        signal, 0, total_rows, device * local_cols, local_cols, total, -1.0, 1.0
+    )
     signal = collect(signal)
     signal = dft_cols(signal, -1.0)
     turned_phase = jnp.transpose(chirp_phase)
     local_phase = lax.all_to_all(
         turned_phase, ("row", "col"), split_axis=0, concat_axis=1, tiled=True
     )
-    signal = complex_product(signal, jnp.cos(local_phase), jnp.sin(local_phase))
+    signal = complex_product(signal, *unit_phase(local_phase))
     signal = dft_cols(signal, 1.0)
-    row_index = device * local_rows + jnp.arange(local_rows, dtype=jnp.int32)
-    col_index = jnp.arange(total_cols, dtype=jnp.int32)
-    signal = rotate(signal, row_index, col_index, total, 1.0, 1.0 / total)
+    signal = rotate(
+        signal, device * local_rows, local_rows, 0, total_cols, total, 1.0, 1.0 / total
+    )
     signal = spread(signal)
     signal = dft_rows(signal, 1.0)
     signal = collect(signal)

time: 2410 us -> 2340 us (0.971)
  local copies, waits for them, and re-layouts: 460 us -> 400 us
  matrix products: 255 us -> 199 us
  waiting for transfers between devices: 1450 us -> 1500 us
    sin x3 -> x1, local copies, waits for them, and re-layouts: 49.8 us -> 0.09 us  [unit_table(): return (factor * jnp.cos(turn), factor * jnp.sin(turn))]
    all_to_all x2, waiting for transfers between devices: 687 us -> 728 us  [collect(): lax.all_to_all(values, ('row', 'col'), split_axis=1, concat_axis=2, tiled...]
    sub x8, other arithmetic: 128 us -> 91.5 us  [complex_product(): real_part = values[0] * cos_part - values[1] * sin_part]
    slice x6 -> x3, local copies, waits for them, and re-layouts: 49 us -> 23.4 us  [complex_product(): real_part = values[0] * cos_part - values[1] * sin_part]
    dot_general x2, matrix products: 63.2 us -> 38.5 us  [dft_cols(): jnp.einsum('cbdq,cmkb->dmqk', dft_table(inner_radix, direction), partial_...]
  transfers between devices with their start and end apart: 6 -> 6, of which waited for: 6 -> 6; matrix products, arithmetic and copies ran while one was open for 11% -> 9% of each run, Pallas kernels for 0% -> 0%
where the time goes in v1:
time: 2340 us; the launch traced here: 2330 us
  waiting for transfers between devices  1500 us (64%)
  local copies, waits for them, and re-layouts  400 us (17%)
  other arithmetic  207 us (9%)
  matrix products  199 us (9%)
  starting transfers between devices  24.2 us (1%)
    all_to_all x2, waiting for transfers between devices, spread(): lax.all_to_all(values, ('row', 'col'), split_axis=2, concat_axis=1, tiled...  748 us
    all_to_all x2, waiting for transfers between devices, collect(): lax.all_to_all(values, ('row', 'col'), split_axis=1, concat_axis=2, tiled...  728 us
    another operation x2, local copies, waits for them, and re-layouts, complex_product(): return jnp.stack([real_part, imag_part])  94.4 us
    sub x8, other arithmetic, complex_product(): real_part = values[0] * cos_part - values[1] * sin_part  91.5 us
    dot_general x3, matrix products, dft_rows(): jnp.einsum('cbdq,ckbm->dqkm', dft_table(inner_radix, direction), partial_...  78.8 us
    dot_general x3, matrix products, dft_rows(): jnp.einsum('cadk,cabm->dkbm', dft_table(outer_radix, direction), blocked,...  54 us
    add x1, other arithmetic, local(): weighted + filter_taps[tap_delay][None, :, None] * turned[:, :, offset:of...  50 us
    all_to_all x3, local copies, waits for them, and re-layouts, collect(): lax.all_to_all(values, ('row', 'col'), split_axis=1, concat_axis=2, tiled...  49.4 us
  transfers between devices with their start and end apart: 6, of which 6 were waited for; matrix products, arithmetic and copies ran while one was open for 9% of the time, Pallas kernels for 0%

profile of v1, /device:TPU:6, one launch (start us, length us, event | category | flops | bytes accessed | tf_op | source)
XLA Modules:
  0.0 2331.8 jit_solution(15980433203493253739)
XLA Ops:
  0.0 24.9 %copy.182 = f32[2,128,16384]{1,0,2:T(2,128)} copy(f32[2,128,16384]{2,1,0:T(8,128)} %param.3) | data formatting | bytes 33554432 | tf_op args[0]
  24.9 6.1 all-to-all-start
  31.0 9.0 copy.194
  40.1 370.0 %all-to-all-done = f32[2,128,16384]{1,0,2:T(2,128)} async-done(((f32[2,128,16384]{1,0,2:T(2,128)}), f32[2,128,16384]{1,0,2:T(2,128)}, u32[]{:S(2)}, u32[]{:S(2)}) %all-to-all-start) | async-done | bytes 16777248 | tf_op jit(solution)/shard_map/all_to_all | solution.py:126
  410.1 3.4 all-to-all-start.2
  415.0 1.0 fusion.80
  416.0 8.2 multiply_subtract_fusion.7
  424.2 20.1 copy.249
  444.3 14.4 fusion.62
  458.7 7.0 multiply_subtract_fusion.8
  465.6 6.4 pad_maximum_fusion
  472.0 26.5 %fusion.50 = f32[2,128,32,512]{3,1,2,0:T(8,128)} fusion(f32[2,32,128,512]{3,1,2,0:T(8,128)} %pad_maximum_fusion, f32[1,128,2,128]{1,3,0,2:T(8,128)S(1)} %get-tuple-element.28, f32[1,128,2,128]{1,3,0,2:T(8,128)S(1)} %get-tuple-element.27), kind=kOutput, calls=%fused_computation.94 | convolution fusion | flops 6442516480 | bytes 33816576 | tf_op jit(solution)/shard_map/cbdq,ckbm->dqkm/dot_general | solution.py:54
  498.5 7.0 fusion.151
  505.6 8.1 copy.185
  513.7 8.3 copy.186
  522.0 19.3 fusion.44
  541.3 6.8 pad_maximum_fusion.1
  548.1 32.2 %copy.187 = f32[2,4096,512]{2,0,1:T(2,128)} copy(f32[2,4096,512]{2,1,0:T(8,128)S(1)} %pad_maximum_fusion.1) | data formatting | bytes 33554432 | tf_op jit(solution)/shard_map/stack | solution.py:31
  580.3 21.4 all-to-all-done.2
  601.7 5.3 all-to-all-start.1
  607.0 0.6 cosine_multiply_fusion
  609.1 8.3 multiply_bitcast_fusion
  617.4 9.0 copy.195
  626.4 9.4 copy.198
  635.8 350.0 %all-to-all-done.1 = f32[2,4096,512]{2,0,1:T(2,128)} async-done(((f32[2,4096,512]{2,0,1:T(2,128)}), f32[2,4096,512]{2,0,1:T(2,128)}, u32[]{:S(2)}, u32[]{:S(2)}) %all-to-all-start.1) | async-done | bytes 16777248 | tf_op jit(solution)/shard_map/all_to_all | solution.py:130
  985.8 14.2 copy.188
  1000.0 17.5 copy.189
  1017.4 18.1 copy.226
  1035.5 13.7 convolution_bitcast_fusion
  1049.3 11.7 multiply_subtract_fusion.6
  1061.0 20.6 fusion.36
  1081.6 17.1 multiply_subtract_fusion.5
  1098.7 14.0 fusion.37
  1112.7 9.6 multiply_subtract_fusion.4
  1122.3 18.0 fusion.40
  1140.3 12.7 multiply_subtract_fusion.2
  1152.9 9.5 copy.206
  1162.4 9.3 copy.207
  1171.7 6.5 pad_maximum_fusion.2
  1178.2 62.1 %copy.208 = f32[2,128,16384]{1,0,2:T(2,128)} copy(f32[2,128,16384]{1,2,0:T(8,128)S(1)} %pad_maximum_fusion.2) | data formatting | bytes 33554432 | tf_op jit(solution)/shard_map/stack | solution.py:31
  1240.3 3.6 all-to-all-start.3
  1244.4 378.0 %all-to-all-done.3 = f32[2,128,16384]{1,0,2:T(2,128)} async-done(((f32[2,128,16384]{1,0,2:T(2,128)}), f32[2,128,16384]{1,0,2:T(2,128)}, u32[]{:S(2)}, u32[]{:S(2)}) %all-to-all-start.3) | async-done | bytes 16777248 | tf_op jit(solution)/shard_map/all_to_all | solution.py:126
  1622.5 20.1 copy.262
  1642.5 14.4 fusion.65
  1656.9 7.0 multiply_subtract_fusion.1
  1663.9 6.4 pad_maximum_fusion.3
  1670.3 26.2 %fusion.53 = f32[2,128,32,512]{3,1,2,0:T(8,128)} fusion(f32[2,32,128,512]{3,1,2,0:T(8,128)} %pad_maximum_fusion.3, f32[1,128,2,128]{1,3,2,0:T(8,128)S(1)} %get-tuple-element.26, f32[1,128,2,128]{1,3,2,0:T(8,128)S(1)} %get-tuple-element.25), kind=kOutput, calls=%fused_computation.95 | convolution fusion | flops 6442516480 | bytes 33816576 | tf_op jit(solution)/shard_map/cbdq,ckbm->dqkm/dot_general | solution.py:54
  1696.4 15.4 copy.213
  1711.9 32.2 %copy.214 = f32[2,4096,512]{2,0,1:T(2,128)} copy(f32[2,4096,512]{2,1,0:T(8,128)S(1)} %bitcast.222) | data formatting | bytes 33554432 | tf_op jit(solution)/shard_map/reshape | solution.py:57
  1744.1 3.8 all-to-all-start.4
  1748.3 377.8 %all-to-all-done.4 = f32[2,4096,512]{2,0,1:T(2,128)} async-done(((f32[2,4096,512]{2,0,1:T(2,128)}), f32[2,4096,512]{2,0,1:T(2,128)}, u32[]{:S(2)}, u32[]{:S(2)}) %all-to-all-start.4) | async-done | bytes 16777248 | tf_op jit(solution)/shard_map/all_to_all | solution.py:130
  2126.1 17.8 copy.294
  2143.9 19.2 reshape_reshape.4
  2163.1 0.8 slice.166
  2164.0 1.9 collective-permute-start
  2166.0 3.5 collective-permute-done
  2169.5 11.8 maximum_bitcast_fusion
  2181.3 50.0 %fusion = f32[2,1024,2048]{1,2,0:T(8,128)} fusion(f32[2,1024,2055]{1,2,0:T(8,128)} %maximum_bitcast_fusion, f32[1024]{0:T(1024)S(1)} %bitcast.239, f32[1024]{0:T(1024)S(1)} %bitcast.240, f32[1024]{0:T(1024)S(1)} %bitcast.234, f32[1024]{0:T(1024)S(1)} %bitcast.235, f32[1024]{0:T(1024)S(1)} %bitcast.236, f32[1024]{0:T(1024)S(1)} %bitcast.237, ...), kind=kLoop, calls=%fused_computation.2 | loop fusion | flops 62914560 | bytes 151027712 | tf_op jit(solution)/shard_map/add | solution.py:172
  2231.4 17.4 copy.216
  2248.8 25.3 %fusion.56 = f32[2,8,128,2048]{3,1,2,0:T(8,128)} fusion(f32[2,8,128,2048]{3,2,1,0:T(8,128)} %bitcast.224, f32[1,8,2,8]{1,3,0,2:T(8,128)S(1)} %copy.180, f32[1,8,2,8]{1,3,0,2:T(8,128)S(1)} %copy.179), kind=kOutput, calls=%fused_computation.96 | convolution fusion | flops 402653440 | bytes 33555456 | tf_op jit(solution)/shard_map/cadk,cabm->dkbm/dot_general | solution.py:49
  2274.1 7.2 multiply_subtract_fusion
  2281.3 6.2 pad_maximum_fusion.4
  2287.6 26.1 %fusion.59 = f32[2,128,8,2048]{3,1,2,0:T(8,128)} fusion(f32[2,8,128,2048]{3,1,2,0:T(8,128)} %pad_maximum_fusion.4, f32[1,128,2,128]{1,3,0,2:T(8,128)S(1)} %copy-done.3, f32[1,128,2,128]{1,3,0,2:T(8,128)S(1)} %copy-done.1), kind=kOutput, calls=%fused_computation.97 | convolution fusion | flops 6442516480 | bytes 33816576 | tf_op jit(solution)/shard_map/cbdq,ckbm->dqkm/dot_general | solution.py:54
  2313.6 18.0 copy.293
  (49 shorter events, 3.9 us)
Async XLA Ops:
  24.9 385.2 %all-to-all-start = ((f32[2,128,16384]{1,0,2:T(2,128)}), f32[2,128,16384]{1,0,2:T(2,128)}, u32[]{:S(2)}, u32[]{:S(2)}) async-start(f32[2,128,16384]{1,0,2:T(2,128)} %copy.182), calls=%async_computation | async-start | bytes 33554432 | tf_op jit(solution)/shard_map/all_to_all | solution.py:126
  410.1 191.7 %all-to-all-start.2 = ((f32[32,128,512]{2,1,0:T(8,128)}), f32[32,128,512]{2,1,0:T(8,128)}, u32[]{:S(2)}, u32[]{:S(2)}) async-start(f32[32,128,512]{2,1,0:T(8,128)} %bitcast.227), calls=%async_computation.2 | async-start | bytes 16777216 | tf_op jit(solution)/shard_map/all_to_all | solution.py:149
  414.6 646.3 %copy-start = (f32[1,128,2,128]{1,3,0,2:T(8,128)}, f32[1,128,2,128]{1,3,0,2:T(8,128)S(1)}, u32[]{:S(2)}) copy-start(f32[1,128,2,128]{1,3,0,2:T(8,128)S(1)} %get-tuple-element.27) | copy-start | bytes 393220
  414.6 646.3 %copy-start.2 = (f32[1,128,2,128]{1,3,0,2:T(8,128)}, f32[1,128,2,128]{1,3,0,2:T(8,128)S(1)}, u32[]{:S(2)}) copy-start(f32[1,128,2,128]{1,3,0,2:T(8,128)S(1)} %get-tuple-element.28) | copy-start | bytes 393220
  601.7 384.0 %all-to-all-start.1 = ((f32[2,4096,512]{2,0,1:T(2,128)}), f32[2,4096,512]{2,0,1:T(2,128)}, u32[]{:S(2)}, u32[]{:S(2)}) async-start(f32[2,4096,512]{2,0,1:T(2,128)} %copy.187), calls=%async_computation.1 | async-start | bytes 33554432 | tf_op jit(solution)/shard_map/all_to_all | solution.py:130
  1049.2 32.3 %slice-start = ((s8[8388608]{0:T(1024)(128)(4,1)}), s8[4194304]{0:T(1024)(128)(4,1)S(1)}, s32[]{:S(2)}) async-start(s8[8388608]{0:T(1024)(128)(4,1)} %bitcast.225), calls=%async_computation.5 | async-start | bytes 8388608
  1061.0 20.6 slice-start.1
  1240.3 382.1 %all-to-all-start.3 = ((f32[2,128,16384]{1,0,2:T(2,128)}), f32[2,128,16384]{1,0,2:T(2,128)}, u32[]{:S(2)}, u32[]{:S(2)}) async-start(f32[2,128,16384]{1,0,2:T(2,128)} %copy.208), calls=%async_computation.3 | async-start | bytes 33554432 | tf_op jit(solution)/shard_map/all_to_all | solution.py:126
  1744.1 4.2 copy-start.4
  1744.1 382.0 %all-to-all-start.4 = ((f32[2,4096,512]{2,0,1:T(2,128)}), f32[2,4096,512]{2,0,1:T(2,128)}, u32[]{:S(2)}, u32[]{:S(2)}) async-start(f32[2,4096,512]{2,0,1:T(2,128)} %copy.214), calls=%async_computation.4 | async-start | bytes 33554432 | tf_op jit(solution)/shard_map/all_to_all | solution.py:130
  2164.0 5.6 collective-permute-start
  2281.3 6.2 copy-start.1
  2281.3 6.2 copy-start.3
